TPU v7x, 128 devices: a whole 4x4x4 slice. The times are simulated.
128 devices in a mesh: lev: 4 (over y), col: 32 (over z, x, core).
Axes of the slice: x: 4, y: 4, z: 4, core: 2. Of those that a mesh axis runs over, the one named last changes fastest.
Arguments:
- control_field: float32 [96, 16, 768, 128], P('lev', None, 'col'), may hold values from -24 to 24
- decay_rate: float32 [96, 768, 128], P('lev', 'col'), may hold values from 0.5 to 0.999
- diffusivity: float32 [768, 128], P('col'), may hold values from 0.08 to 0.24
Outputs:
- localized: float32 [96, 16, 768, 128], P('lev', None, 'col')
All inputs are finite; a program needn't handle non-finite values.
Results may differ from a plain program's by a relative error of at most 0.00002.
Values sent between devices are 32-bit elements; how exact they have to be, the bound alone decides.
A program may use at most 64 MiB of HBM per device.

v0:
```python
import jax
import jax.numpy as jnp
from jax import lax
from jax.sharding import PartitionSpec as P

SMOOTH = 4


def sent_to_all(x, axis):
    peers = lax.axis_size(axis)
    return lax.all_to_all(jnp.broadcast_to(x[None], (peers, *x.shape)), axis, 0, 0, tiled=True)


def combined_pairwise(pieces, combine):
    while len(jax.tree.leaves(pieces)[0]) > 1:
        pieces = jax.vmap(combine)(
            *(jax.tree.map(lambda part: part[side::2], pieces) for side in (0, 1))
        )
    return jax.tree.map(lambda part: part[0], pieces)


def prefix(x, axis, combine, identity, reverse):
    peers, here = (lax.axis_size(axis), lax.axis_index(axis))
    passed = jnp.arange(peers) > here if reverse else jnp.arange(peers) < here

    def kept(part, zero, own):
        part = jnp.where(
            passed.reshape(-1, *(1 for _ in own.shape)), part, jnp.asarray(zero, own.dtype)
        )
        return part[::-1] if reverse else part

    pieces = jax.tree.map(lambda part: sent_to_all(part, axis), x)
    return combined_pairwise(jax.tree.map(kept, pieces, identity, x), combine)


def with_halo(block, sides, width):
    for axis, dim in sides:
        count = lax.axis_size(axis)
        forward = [(i, i + 1) for i in range(count - 1)]
        backward = [(target, source) for source, target in forward]
        low = lax.ppermute(
            lax.slice_in_dim(block, block.shape[dim] - width, None, axis=dim), axis, forward
        )
        high = lax.ppermute(lax.slice_in_dim(block, 0, width, axis=dim), axis, backward)
        block = jnp.concatenate([low, block, high], axis=dim)
    return block


def sweep_levels(decay_rates, field, backward):
    blocks = field.shape[0] // 8
    rate_blocks = decay_rates.reshape((blocks, 8) + decay_rates.shape[1:])
    field_blocks = field.reshape((blocks, 8) + field.shape[1:])

    def run_block(state, inputs):
        rate_block, values_block = inputs
        results = [None] * 8
        order = range(7, -1, -1) if backward else range(8)
        for position in order:
            weight = rate_block[position]
            state = weight * state + (1.0 - weight) * values_block[position]
            results[position] = state
        return (state, jnp.stack(results))

    start = jnp.zeros(field.shape[1:], jnp.float32)
    unused, swept = lax.scan(run_block, start, (rate_blocks, field_blocks), reverse=backward)
    return swept.reshape(field.shape)


def combine_maps(earlier, later):
    return (later[0] * earlier[0], later[0][None] * earlier[1] + later[1])


def forward_pass(decay_rates, field):
    within = sweep_levels(decay_rates, field, False)
    through = jnp.prod(decay_rates, axis=0)
    identity = (jnp.ones_like(through), jnp.zeros_like(within[-1]))
    entering = prefix((through, within[-1]), "lev", combine_maps, identity, False)
    growth = jnp.cumprod(decay_rates, axis=0)
    return within + growth[:, None] * entering[1][None]


def backward_pass(decay_rates, field):
    within = sweep_levels(decay_rates, field, True)
    through = jnp.prod(decay_rates, axis=0)
    identity = (jnp.ones_like(through), jnp.zeros_like(within[0]))
    entering = prefix((through, within[0]), "lev", combine_maps, identity, True)
    growth = jnp.flip(jnp.cumprod(jnp.flip(decay_rates, 0), axis=0), 0)
    return within + growth[:, None] * entering[1][None]


def lat_sum(field):
    padded = jnp.pad(field, ((0, 0), (0, 0), (0, 0), (1, 1)))
    return padded[..., 2:] + padded[..., :-2]


def per_device(control_field, decay_rate, diffusivity):
    filtered = control_field
    for repeat in range(2):
        filtered = forward_pass(decay_rate, filtered)
        filtered = backward_pass(decay_rate, filtered)
    current = with_halo(filtered, (("col", 2),), SMOOTH)
    kappa_wide = with_halo(diffusivity, (("col", 0),), SMOOTH)
    for position in range(SMOOTH):
        center = current[:, :, 1:-1]
        kappa_part = kappa_wide[position + 1 : kappa_wide.shape[0] - position - 1]
        current = center + kappa_part[None, None] * (
            current[:, :, 2:] + current[:, :, :-2] + lat_sum(center) - 4.0 * center
        )
    return current


def solution(mesh):
    in_specs = (P("lev", None, "col", None), P("lev", "col", None), P("col", None))
    out_specs = P("lev", None, "col", None)
    return jax.shard_map(
        per_device, mesh=mesh, in_specs=in_specs, out_specs=out_specs, check_vma=False
    )
```

profile of v0, /device:TPU:7, one launch (start us, length us, event | category | flops | bytes accessed | tf_op | source)
XLA Modules:
  0.0 229.9 jit_solution(5336159888158184857)
XLA Ops:
  1.7 4.2 %all-to-all-start = ((f32[4,24,128]{2,1,0:T(8,128)}), f32[4,24,128]{2,1,0:T(8,128)S(1)}, u32[]{:S(2)}, u32[]{:S(2)}) async-start(f32[4,24,128]{2,1,0:T(8,128)} %broadcast_in_dim.172), calls=%async_computation | async-start | bytes 98304 | tf_op jit(solution)/shard_map/all_to_all | solution.py:11
  6.9 2.7 %broadcast.243.clone.2 = f32[3,8,16,24,128]{4,3,2,1,0:T(8,128)} broadcast(f32[]{:T(128)} %constant.132.clone.1), dimensions={} | broadcast | bytes 4718596 | tf_op jit(solution)/shard_map/broadcast.12
  9.6 28.4 %while.60 = (s32[]{:T(128)}, f32[16,24,128]{2,1,0:T(8,128)S(1)}, f32[3,8,16,24,128]{4,3,2,1,0:T(8,128)}, f32[3,8,24,128]{3,2,1,0:T(8,128)S(1)}, f32[3,8,16,24,12...) while((s32[]{:T(128)}, f32[16,24,128]{2,1,0:T(8,128)S(1)}, ...), condition=%wide.region_1.2_spmd.clone, body=%wide.region_0.1_spmd.clone.sunk | while | flops 1695753 | bytes 10003275 | solution.py:65
  40.0 4.2 %all-to-all-start.1 = ((f32[4,16,24,128]{3,1,2,0:T(8,128)}), f32[4,16,24,128]{3,1,2,0:T(8,128)S(1)}, u32[]{:S(2)}, u32[]{:S(2)}) async-start(f32[4,16,24,128]{3,1,2,0:T(8,128)} %broadcast_in_dim.176), calls=%async_computation.1 | async-start | bytes 1572864 | tf_op jit(solution)/shard_map/all_to_all | solution.py:11
  44.3 10.8 %all-to-all-done.1 = f32[4,16,24,128]{3,1,2,0:T(8,128)S(1)} async-done(((f32[4,16,24,128]{3,1,2,0:T(8,128)}), f32[4,16,24,128]{3,1,2,0:T(8,128)S(1)}, u32[]{:S(2)}, u32[]{:S(2)}) %all-to-all-start.1) | async-done | bytes 786464 | tf_op jit(solution)/shard_map/all_to_all | solution.py:11
  55.4 5.2 %multiply_add_fusion.3 = f32[3,8,16,24,128]{4,3,2,1,0:T(8,128)} fusion(f32[3,8,16,24,128]{4,3,2,1,0:T(8,128)} %get-tuple-element.265, f32[16,24,128]{2,1,0:T(8,128)S(1)} %copy.7, f32[3,8,24,128]{3,2,1,0:T(8,128)S(1)} %bitcast.578), kind=kLoop, calls=%fused_computation.236 | loop fusion | flops 2359296 | bytes 9928704 | tf_op jit(solution)/shard_map/add | solution.py:79
  60.6 2.7 %broadcast.243.clone.1 = f32[3,8,16,24,128]{4,3,2,1,0:T(8,128)} broadcast(f32[]{:T(128)} %constant.132.clone.1), dimensions={} | broadcast | bytes 4718596 | tf_op jit(solution)/shard_map/broadcast.12
  63.3 18.0 %while.61 = (s32[]{:T(128)}, f32[16,24,128]{2,1,0:T(8,128)S(1)}, f32[3,8,16,24,128]{4,3,2,1,0:T(8,128)}, f32[3,8,24,128]{3,2,1,0:T(8,128)S(1)}, f32[3,8,16,24,12...) while((s32[]{:T(128)}, f32[16,24,128]{2,1,0:T(8,128)S(1)}, ...), condition=%wide.region_5.6_spmd.clone, body=%wide.region_4.5_spmd.clone.sunk | while | flops 1695754 | bytes 10002771 | solution.py:65
  83.2 3.5 %all-to-all-start.2 = ((f32[4,16,24,128]{3,1,2,0:T(8,128)}), f32[4,16,24,128]{3,1,2,0:T(8,128)S(1)}, u32[]{:S(2)}, u32[]{:S(2)}) async-start(f32[4,16,24,128]{3,1,2,0:T(8,128)} %broadcast_in_dim.181), calls=%async_computation.2 | async-start | bytes 1572864 | tf_op jit(solution)/shard_map/all_to_all | solution.py:11
  88.1 8.3 %all-to-all-done.2 = f32[4,16,24,128]{3,1,2,0:T(8,128)S(1)} async-done(((f32[4,16,24,128]{3,1,2,0:T(8,128)}), f32[4,16,24,128]{3,1,2,0:T(8,128)S(1)}, u32[]{:S(2)}, u32[]{:S(2)}) %all-to-all-start.2) | async-done | bytes 786464 | tf_op jit(solution)/shard_map/all_to_all | solution.py:11
  101.4 2.7 %broadcast.243 = f32[3,8,16,24,128]{4,3,2,1,0:T(8,128)} broadcast(f32[]{:T(128)} %constant.132.clone.1), dimensions={} | broadcast | bytes 4718596 | tf_op jit(solution)/shard_map/broadcast.12
  104.2 28.4 %while.62 = (s32[]{:T(128)}, f32[16,24,128]{2,1,0:T(8,128)S(1)}, f32[3,8,16,24,128]{4,3,2,1,0:T(8,128)}, f32[3,8,24,128]{3,2,1,0:T(8,128)S(1)}, f32[3,8,16,24,12...) while((s32[]{:T(128)}, f32[16,24,128]{2,1,0:T(8,128)S(1)}, ...), condition=%wide.region_8.9_spmd.clone, body=%wide.region_7.8_spmd.clone.sunk | while | flops 1695753 | bytes 10003275 | solution.py:65
  134.5 3.5 %all-to-all-start.3 = ((f32[4,16,24,128]{3,1,2,0:T(8,128)}), f32[4,16,24,128]{3,1,2,0:T(8,128)S(1)}, u32[]{:S(2)}, u32[]{:S(2)}) async-start(f32[4,16,24,128]{3,1,2,0:T(8,128)} %broadcast_in_dim.183), calls=%async_computation.3 | async-start | bytes 1572864 | tf_op jit(solution)/shard_map/all_to_all | solution.py:11
  138.0 8.5 %all-to-all-done.3 = f32[4,16,24,128]{3,1,2,0:T(8,128)S(1)} async-done(((f32[4,16,24,128]{3,1,2,0:T(8,128)}), f32[4,16,24,128]{3,1,2,0:T(8,128)S(1)}, u32[]{:S(2)}, u32[]{:S(2)}) %all-to-all-start.3) | async-done | bytes 786464 | tf_op jit(solution)/shard_map/all_to_all | solution.py:11
  146.8 5.2 %multiply_add_fusion.1 = f32[3,8,16,24,128]{4,3,2,1,0:T(8,128)} fusion(f32[3,8,16,24,128]{4,3,2,1,0:T(8,128)} %get-tuple-element.267, f32[16,24,128]{2,1,0:T(8,128)S(1)} %copy.11, f32[3,8,24,128]{3,2,1,0:T(8,128)S(1)} %bitcast.579), kind=kLoop, calls=%fused_computation.234 | loop fusion | flops 2359296 | bytes 9928704 | tf_op jit(solution)/shard_map/add | solution.py:79
  154.7 18.5 %while.63 = (s32[]{:T(128)}, f32[16,24,128]{2,1,0:T(8,128)S(1)}, f32[3,8,16,24,128]{4,2,3,1,0:T(8,128)}, f32[3,8,24,128]{3,2,1,0:T(8,128)S(1)}, f32[3,8,16,24,12...) while((s32[]{:T(128)}, f32[16,24,128]{2,1,0:T(8,128)S(1)}, ...), condition=%wide.region_10.11_spmd.clone, body=%wide.region_9.10_spmd.clone.sunk | while | flops 1695754 | bytes 10002771 | solution.py:65
  174.3 10.9 %all_to_all.28 = f32[4,16,24,128]{3,1,2,0:T(8,128)S(1)} all-to-all(f32[4,16,24,128]{3,1,2,0:T(8,128)S(1)} %broadcast_in_dim.185), channel_id=1, replica_groups=mesh['lev'=4,'col'=32] {'lev'}, dimensions={0} | all-to-all | bytes 1572864 | tf_op jit(solution)/shard_map/all_to_all | solution.py:11
  186.5 9.2 %collective-permute-start = (f32[24,16,4,128]{3,1,2,0:T(8,128)S(1)}, f32[24,16,4,128]{3,1,2,0:T(8,128)S(1)}, u32[]{:S(2)}, u32[]{:S(2)}) collective-permute-start(f32[24,16,4,128]{3,1,2,0:T(8,128)S(1)} %get-tuple-element.533), channel_id=1, source_target_pairs={{0,1},{1,2},{2,3},{3,4},{4,5},{5,6},{6,7},{7,8},{8,9},{9,10},{10,1... | collective-permute-start | bytes 2359304 | tf_op jit(solution)/shard_map/ppermute | solution.py:41
  197.7 5.8 %collective-permute-start.2 = (f32[4,128]{1,0:T(4,128)S(1)}, f32[4,128]{1,0:T(4,128)S(1)}, u32[]{:S(2)}, u32[]{:S(2)}) collective-permute-start(f32[4,128]{1,0:T(4,128)S(1)} %get-tuple-element.545), channel_id=1, source_target_pairs={{0,1},{1,2},{2,3},{3,4},{4,5},{5,6},{6,7},{7,8},{8,9},{9,10},{10,1... | collective-permute-start | bytes 6152 | tf_op jit(solution)/shard_map/ppermute | solution.py:41
  205.5 5.6 %collective-permute-done.3 = f32[4,128]{1,0:T(4,128)S(1)} collective-permute-done((f32[4,128]{1,0:T(4,128)S(1)}, f32[4,128]{1,0:T(4,128)S(1)}, u32[]{:S(2)}, u32[]{:S(2)}) %collective-permute-start.3) | collective-permute-done | bytes 2080 | tf_op jit(solution)/shard_map/ppermute | solution.py:44
  212.4 3.2 %fusion.68 = f32[24,16,30,128]{3,1,2,0:T(8,128)S(1)} fusion(f32[24,16,30,128]{3,1,2,0:T(8,128)S(1)} %slice.782, f32[24,16,32,128]{3,1,2,0:T(8,128)S(1)} %pad_maximum_fusion, f32[30,128]{1,0:T(8,128)S(1)} %slice.783), kind=kLoop, calls=%fused_computation.213 | loop fusion | flops 10321920 | bytes 23608320 | tf_op jit(solution)/shard_map/add | solution.py:106
  216.1 3.0 %fusion.73 = f32[24,16,28,128]{3,1,2,0:T(8,128)S(1)} fusion(f32[24,16,28,128]{3,1,2,0:T(8,128)S(1)} %slice.786, f32[24,16,30,128]{3,1,2,0:T(8,128)S(1)} %fusion.68, f32[28,128]{1,0:T(8,128)S(1)} %slice.787), kind=kLoop, calls=%fused_computation.219 | loop fusion | flops 9633792 | bytes 22034432 | tf_op jit(solution)/shard_map/add | solution.py:106
  219.6 3.2 %fusion.78 = f32[24,16,26,128]{3,1,2,0:T(8,128)S(1)} fusion(f32[24,16,26,128]{3,1,2,0:T(8,128)S(1)} %slice.790, f32[24,16,28,128]{3,1,2,0:T(8,128)S(1)} %fusion.73, f32[26,128]{1,0:T(8,128)S(1)} %slice.791), kind=kLoop, calls=%fused_computation.225 | loop fusion | flops 8945664 | bytes 20460544 | tf_op jit(solution)/shard_map/add | solution.py:106
  225.9 4.0 %copy.13 = f32[24,16,24,128]{3,2,1,0:T(8,128)} copy(f32[24,16,24,128]{3,1,2,0:T(8,128)S(1)} %fusion.83) | data formatting | bytes 9437184 | tf_op jit(solution)/shard_map/add | solution.py:106
  (196 shorter events, 122.6 us)
Async XLA Ops:
  0.0 9.6 %copy-start = (f32[24,24,128]{2,1,0:T(8,128)S(1)}, f32[24,24,128]{2,1,0:T(8,128)}, u32[]{:S(2)}) copy-start(f32[24,24,128]{2,1,0:T(8,128)} %param.12) | copy-start | bytes 884740
  1.7 37.3 %all-to-all-start = ((f32[4,24,128]{2,1,0:T(8,128)}), f32[4,24,128]{2,1,0:T(8,128)S(1)}, u32[]{:S(2)}, u32[]{:S(2)}) async-start(f32[4,24,128]{2,1,0:T(8,128)} %broadcast_in_dim.172), calls=%async_computation | async-start | bytes 98304 | tf_op jit(solution)/shard_map/all_to_all | solution.py:11
  40.0 15.1 %all-to-all-start.1 = ((f32[4,16,24,128]{3,1,2,0:T(8,128)}), f32[4,16,24,128]{3,1,2,0:T(8,128)S(1)}, u32[]{:S(2)}, u32[]{:S(2)}) async-start(f32[4,16,24,128]{3,1,2,0:T(8,128)} %broadcast_in_dim.176), calls=%async_computation.1 | async-start | bytes 1572864 | tf_op jit(solution)/shard_map/all_to_all | solution.py:11
  83.2 13.2 %all-to-all-start.2 = ((f32[4,16,24,128]{3,1,2,0:T(8,128)}), f32[4,16,24,128]{3,1,2,0:T(8,128)S(1)}, u32[]{:S(2)}, u32[]{:S(2)}) async-start(f32[4,16,24,128]{3,1,2,0:T(8,128)} %broadcast_in_dim.181), calls=%async_computation.2 | async-start | bytes 1572864 | tf_op jit(solution)/shard_map/all_to_all | solution.py:11
  96.4 2.3 %copy-start.2 = (f32[3,8,16,24,128]{4,3,2,1,0:T(8,128)S(1)}, f32[3,8,16,24,128]{4,3,2,1,0:T(8,128)}, u32[]{:S(2)}) copy-start(f32[3,8,16,24,128]{4,3,2,1,0:T(8,128)} %get-tuple-element.266) | copy-start | bytes 14155780
  134.5 12.0 %all-to-all-start.3 = ((f32[4,16,24,128]{3,1,2,0:T(8,128)}), f32[4,16,24,128]{3,1,2,0:T(8,128)S(1)}, u32[]{:S(2)}, u32[]{:S(2)}) async-start(f32[4,16,24,128]{3,1,2,0:T(8,128)} %broadcast_in_dim.183), calls=%async_computation.3 | async-start | bytes 1572864 | tf_op jit(solution)/shard_map/all_to_all | solution.py:11
  173.2 12.4 %copy-start.1 = (f32[3,8,16,24,128]{4,2,3,1,0:T(8,128)S(1)}, f32[3,8,16,24,128]{4,2,3,1,0:T(8,128)}, u32[]{:S(2)}) copy-start(f32[3,8,16,24,128]{4,2,3,1,0:T(8,128)} %get-tuple-element.268) | copy-start | bytes 14155780
  185.5 12.1 %copy-start.3 = (f32[24,128]{1,0:T(8,128)S(1)}, f32[24,128]{1,0:T(8,128)}, u32[]{:S(2)}) copy-start(f32[24,128]{1,0:T(8,128)} %param.13) | copy-start | bytes 36868
  186.5 24.7 %collective-permute-start = (f32[24,16,4,128]{3,1,2,0:T(8,128)S(1)}, f32[24,16,4,128]{3,1,2,0:T(8,128)S(1)}, u32[]{:S(2)}, u32[]{:S(2)}) collective-permute-start(f32[24,16,4,128]{3,1,2,0:T(8,128)S(1)} %get-tuple-element.533), channel_id=1, source_target_pairs={{0,1},{1,2},{2,3},{3,4},{4,5},{5,6},{6,7},{7,8},{8,9},{9,10},{10,1... | collective-permute-start | bytes 2359304 | tf_op jit(solution)/shard_map/ppermute | solution.py:41
  195.7 15.5 %collective-permute-start.1 = (f32[24,16,4,128]{3,1,2,0:T(8,128)S(1)}, f32[24,16,4,128]{3,1,2,0:T(8,128)S(1)}, u32[]{:S(2)}, u32[]{:S(2)}) collective-permute-start(f32[24,16,4,128]{3,1,2,0:T(8,128)S(1)} %get-tuple-element.534), channel_id=1, source_target_pairs={{1,0},{2,1},{3,2},{4,3},{5,4},{6,5},{7,6},{8,7},{9,8},{10,9},{11,1... | collective-permute-start | bytes 2359304 | tf_op jit(solution)/shard_map/ppermute | solution.py:44
  197.7 7.9 %collective-permute-start.2 = (f32[4,128]{1,0:T(4,128)S(1)}, f32[4,128]{1,0:T(4,128)S(1)}, u32[]{:S(2)}, u32[]{:S(2)}) collective-permute-start(f32[4,128]{1,0:T(4,128)S(1)} %get-tuple-element.545), channel_id=1, source_target_pairs={{0,1},{1,2},{2,3},{3,4},{4,5},{5,6},{6,7},{7,8},{8,9},{9,10},{10,1... | collective-permute-start | bytes 6152 | tf_op jit(solution)/shard_map/ppermute | solution.py:41
  203.4 7.7 %collective-permute-start.3 = (f32[4,128]{1,0:T(4,128)S(1)}, f32[4,128]{1,0:T(4,128)S(1)}, u32[]{:S(2)}, u32[]{:S(2)}) collective-permute-start(f32[4,128]{1,0:T(4,128)S(1)} %get-tuple-element.546), channel_id=1, source_target_pairs={{1,0},{2,1},{3,2},{4,3},{5,4},{6,5},{7,6},{8,7},{9,8},{10,9},{11,1... | collective-permute-start | bytes 6152 | tf_op jit(solution)/shard_map/ppermute | solution.py:44
where the time goes:
time: 232 us; the launch traced here: 230 us
  other arithmetic  107 us (46%)
  local copies, waits for them, and re-layouts  43 us (19%)
  starting transfers between devices  34.4 us (15%)
  waiting for transfers between devices  33.2 us (14%)
  blocking collectives  10.9 us (5%)
    while x66, other arithmetic  70.6 us
    all_to_all x4, waiting for transfers between devices, sent_to_all(): lax.all_to_all(jnp.broadcast_to(x[None], (peers, *x.shape)), axis, 0, 0,...  27.6 us
    dynamic_update_slice x12, local copies, waits for them, and re-layouts, sweep_levels(): lax.scan(run_block, start, (rate_blocks, field_blocks), reverse=backward)  15.7 us
    all_to_all x4, starting transfers between devices, sent_to_all(): lax.all_to_all(jnp.broadcast_to(x[None], (peers, *x.shape)), axis, 0, 0,...  15.4 us
    ppermute x2, starting transfers between devices, with_halo(): lax.ppermute(lax.slice_in_dim(block, block.shape[dim] - width, None, axis...  14.9 us
    add x4, other arithmetic, per_device(): center + kappa_part[None, None] * (current[:, :, 2:] + current[:, :, :-2]...  12 us
    all_to_all x1, blocking collectives, sent_to_all(): lax.all_to_all(jnp.broadcast_to(x[None], (peers, *x.shape)), axis, 0, 0,...  10.9 us
    another operation x4, local copies, waits for them, and re-layouts  10.9 us
  transfers between devices with their start and end apart: 8, of which 4 were waited for; matrix products, arithmetic and copies ran while one was open for 15% of the time, Pallas kernels for 0%

commit v1 on v0

v1 whole, which is shorter than its diff:
```python
import functools

import jax
import jax.numpy as jnp
from jax import lax
from jax.experimental import pallas as pl
from jax.experimental.pallas import tpu as pltpu
from jax.sharding import PartitionSpec as P

MESH = pl.DeviceIdType.MESH
SMOOTH = 4
PAIR = 2
LAG = 6
HALO_LAG = 6


def kernel(n_lev, n_col, x_hbm, w_hbm, kap_ref, y_ref, wv, bv, G, C, E, rin, rout, qin, qout, hs, hin, U, T, ks, kin, kw,
           kc, wsem, xsem, rsend, rrecv, qsend, qrecv, hsend, hrecv, ksend, krecv):
    levels, members, lons, lats = x_hbm.shape
    d, c = lax.axis_index("lev"), lax.axis_index("col")
    has_low, has_high = d > 0, d < n_lev - 1
    has_left, has_right = c > 0, c < n_col - 1
    middle = jnp.logical_and(has_low, has_high)

    barrier = pltpu.get_barrier_semaphore()
    for there, where in ((has_low, {"lev": d - 1}), (has_high, {"lev": d + 1}), (has_left, {"col": c - 1}), (has_right, {"col": c + 1})):
        @pl.when(there)
        def _():
            pl.semaphore_signal(barrier, inc=1, device_id=where, device_id_type=MESH)

    w_copy = pltpu.make_async_copy(w_hbm, wv, wsem)
    w_copy.start()

    def x_copy(m):
        return pltpu.make_async_copy(x_hbm.at[:, m], y_ref.at[m], xsem.at[m])

    for m in range(members):
        x_copy(m).start()

    def r_copy(u, src):
        return pltpu.make_async_remote_copy(src, rin.at[u], rsend.at[u], rrecv.at[u], device_id={"lev": d + 1}, device_id_type=MESH)

    def q_copy(u, src):
        return pltpu.make_async_remote_copy(src, qin.at[u], qsend.at[u], qrecv.at[u], device_id={"lev": d - 1}, device_id_type=MESH)

    def left_copy(m):
        return pltpu.make_async_remote_copy(hs.at[m, 0], hin.at[m, 1], hsend.at[m, 0], hrecv.at[m, 1], device_id={"col": c - 1}, device_id_type=MESH)

    def right_copy(m):
        return pltpu.make_async_remote_copy(hs.at[m, 1], hin.at[m, 0], hsend.at[m, 1], hrecv.at[m, 0], device_id={"col": c + 1}, device_id_type=MESH)

    def kleft_copy():
        return pltpu.make_async_remote_copy(ks.at[0], kin.at[1], ksend.at[0], krecv.at[1], device_id={"col": c - 1}, device_id_type=MESH)

    def kright_copy():
        return pltpu.make_async_remote_copy(ks.at[1], kin.at[0], ksend.at[1], krecv.at[0], device_id={"col": c + 1}, device_id_type=MESH)

    @pl.when(d == 0)
    def _():
        rin[...] = jnp.zeros_like(rin)

    @pl.when(d == n_lev - 1)
    def _():
        qin[...] = jnp.zeros_like(qin)

    @pl.when(c == 0)
    def _():
        kin[0] = jnp.zeros(kin.shape[1:], jnp.float32)
        hin[:, 0] = jnp.zeros((members,) + hin.shape[2:], jnp.float32)

    @pl.when(c == n_col - 1)
    def _():
        kin[1] = jnp.zeros(kin.shape[1:], jnp.float32)
        hin[:, 1] = jnp.zeros((members,) + hin.shape[2:], jnp.float32)

    ks[...] = jnp.zeros_like(ks)
    ks[0, 0:SMOOTH] = kap_ref[0:SMOOTH]
    ks[1, 0:SMOOTH] = kap_ref[lons - SMOOTH : lons]

    w_copy.wait()
    state = jnp.ones((lons, lats), jnp.float32)
    for k in range(levels):
        bv[k] = 1.0 - wv[k]
        state = state * wv[k]
        G[0, k] = state
    C[0] = state
    state = jnp.ones((lons, lats), jnp.float32)
    for k in reversed(range(levels)):
        state = state * wv[k]
        G[3, k] = state

    def forward(src, dst):
        state = jnp.zeros((lons, lats), jnp.float32)
        for k in range(levels):
            state = wv[k] * state + bv[k] * G[src, k]
            G[dst, k] = state
        return state

    def backward(src, dst):
        state = jnp.zeros((lons, lats), jnp.float32)
        for k in reversed(range(levels)):
            state = wv[k] * state + bv[k] * G[src, k]
            G[dst, k] = state
        return state

    C[1] = backward(0, 2)
    C[2] = forward(3, 1)
    C[3] = forward(2, 0)
    C[4] = backward(0, 0)
    C[5] = backward(1, 1)
    p, cc, a, e, g, h = (C.at[i] for i in range(6))

    pl.semaphore_wait(barrier, sum(there.astype(jnp.int32) for there in (has_low, has_high, has_left, has_right)))

    @pl.when(d == 0)
    def _():
        rout[0, 0] = a[...]
        rout[0, 1] = a[...]
        r_copy(0, rout.at[0]).start()

    @pl.when(d == n_lev - 1)
    def _():
        qout[0, 0] = cc[...]
        qout[0, 1] = g[...]
        q_copy(0, qout.at[0]).start()

    @pl.when(has_left)
    def _():
        kleft_copy().start()

    @pl.when(has_right)
    def _():
        kright_copy().start()

    @pl.loop(0, members // PAIR)
    def _(i):
        first = i * PAIR
        for j in range(PAIR):
            x_copy(first + j).wait()
        for order, slot in ((range(levels), 0), (range(levels - 1, -1, -1), 2), (range(levels), 1), (range(levels - 1, -1, -1), 3)):
            states = [jnp.zeros((lons, lats), jnp.float32)] * PAIR
            for k in order:
                weight, rest = wv[k], bv[k]
                for j in range(PAIR):
                    states[j] = weight * states[j] + rest * y_ref[first + j, k]
                    y_ref[first + j, k] = states[j]
            for j in range(PAIR):
                E[first + j, slot] = states[j]

        @pl.when(d == 0)
        def _():
            for j in range(PAIR):
                r_copy(first + j + 1, E.at[first + j, pl.ds(0, 2)]).start()

        @pl.when(d == n_lev - 1)
        def _():
            for j in range(PAIR):
                q_copy(first + j + 1, E.at[first + j, pl.ds(2, 2)]).start()

    @pl.when(has_left)
    def _():
        kright = pltpu.make_async_remote_copy(ks.at[1], kin.at[0], ksend.at[1], krecv.at[0], device_id={"col": c - 1}, device_id_type=MESH)
        kright.wait_recv()

    @pl.when(has_right)
    def _():
        kleft = pltpu.make_async_remote_copy(ks.at[0], kin.at[1], ksend.at[0], krecv.at[1], device_id={"col": c + 1}, device_id_type=MESH)
        kleft.wait_recv()

    kw[...] = jnp.zeros_like(kw)
    kw[8 - SMOOTH : 8] = kin[0, 0:SMOOTH]
    kw[8 : 8 + lons] = kap_ref[...]
    kw[8 + lons : 8 + lons + SMOOTH] = kin[1, 0:SMOOTH]
    kappa = kw[...]
    lane = lax.broadcasted_iota(jnp.int32, kappa.shape, 1)
    kc[0] = 1.0 - 4.0 * kappa
    kc[1] = jnp.where(lane > 0, kappa, 0.0)
    kc[2] = jnp.where(lane < lats - 1, kappa, 0.0)

    def r_wait(u):
        r_copy(u, rout.at[u]).wait_recv()

    def q_wait(u):
        q_copy(u, qout.at[u]).wait_recv()

    def r_forward(u):
        r_wait(u)

        @pl.when(u == 0)
        def _():
            rho = a[...] + p[...] * p[...] * rin[0, 0]
            rout[0, 0] = rho
            rout[0, 1] = rho

        @pl.when(u > 0)
        def _():
            m = u - 1
            f1_in, f2_in = rin[u, 0], rin[u, 1]
            b1_out = E[m, 2] + cc[...] * f1_in
            f2_in = f2_in + rin[0, 0] * b1_out
            rout[u, 0] = E[m, 0] + p[...] * f1_in
            rout[u, 1] = E[m, 1] + p[...] * f2_in + e[...] * f1_in

        r_copy(u, rout.at[u]).start()

    def q_forward(u):
        q_wait(u)

        @pl.when(u == 0)
        def _():
            k1, k2 = qin[0, 0], qin[0, 1]
            qout[0, 0] = cc[...] + p[...] * p[...] * k1
            qout[0, 1] = g[...] + p[...] * (h[...] * k1 + p[...] * k2 + k1 * (e[...] + a[...] * p[...] * k1))

        @pl.when(u > 0)
        def _():
            m = u - 1
            k1, k2 = qin[0, 0], qin[0, 1]
            f1 = E[m, 0]
            b1_in = qin[u, 0] + k1 * f1
            f2 = E[m, 1] + a[...] * b1_in
            b2_in = qin[u, 1] + k2 * f1 + k1 * f2
            qout[u, 0] = E[m, 2] + p[...] * b1_in
            qout[u, 1] = E[m, 3] + p[...] * b2_in + h[...] * b1_in

        q_copy(u, qout.at[u]).start()

    def finish(m):
        u = m + 1
        for t in range(lons // 8):
            rows = pl.ds(8 * t, 8)
            rho, k1, k2 = rin[0, 0, rows], qin[0, 0, rows], qin[0, 1, rows]
            pp, c1, aa, ee = p[rows], cc[rows], a[rows], e[rows]
            f1_in = rin[u, 0, rows]
            f1 = E[m, 0, rows] + pp * f1_in
            b1_in = qin[u, 0, rows] + k1 * f1
            b1 = E[m, 2, rows] + c1 * f1_in + pp * b1_in
            f2_in = rin[u, 1, rows] + rho * b1
            f2 = E[m, 1, rows] + pp * f2_in + ee * f1_in + aa * b1_in
            b2_in = qin[u, 1, rows] + k2 * f1 + k1 * f2
            for k in range(levels):
                value = y_ref[m, k, rows] + (G[0, k, rows] * f1_in + G[1, k, rows] * b1_in) + (G[2, k, rows] * f2_in + G[3, k, rows] * b2_in)
                U[m, k, 8 + 8 * t : 16 + 8 * t] = value
                if t == 0:
                    hs[m, 0, SMOOTH * k : SMOOTH * (k + 1)] = value[0:SMOOTH]
                if t == lons // 8 - 1:
                    hs[m, 1, SMOOTH * k : SMOOTH * (k + 1)] = value[8 - SMOOTH : 8]

        @pl.when(has_left)
        def _():
            left_copy(m).start()

        @pl.when(has_right)
        def _():
            right_copy(m).start()

    def diffuse(m):
        @pl.when(has_left)
        def _():
            pltpu.make_async_remote_copy(hs.at[m, 1], hin.at[m, 0], hsend.at[m, 1], hrecv.at[m, 0], device_id={"col": c - 1}, device_id_type=MESH).wait_recv()

        @pl.when(has_right)
        def _():
            pltpu.make_async_remote_copy(hs.at[m, 0], hin.at[m, 1], hsend.at[m, 0], hrecv.at[m, 1], device_id={"col": c + 1}, device_id_type=MESH).wait_recv()

        for k in range(levels):
            U[m, k, 8 - SMOOTH : 8] = hin[m, 0, SMOOTH * k : SMOOTH * (k + 1)]
            U[m, k, 8 + lons : 8 + lons + SMOOTH] = hin[m, 1, SMOOTH * k : SMOOTH * (k + 1)]
        for s in range(SMOOTH):
            src = U.at[m] if s % 2 == 0 else T
            dst = T if s % 2 == 0 else U.at[m]
            last = s == SMOOTH - 1
            start = 8 - SMOOTH + 1 + s
            tiles = lons // 8 + (0 if last else 1)
            for t in range(tiles):
                row = start + 8 * t
                keep, north, south, both = kc[0, row : row + 8], kc[1, row : row + 8], kc[2, row : row + 8], kw[row : row + 8]
                for k in range(levels):
                    center = src[k, row : row + 8]
                    value = keep * center + both * (src[k, row - 1 : row + 7] + src[k, row + 1 : row + 9])
                    value = value + (north * pltpu.roll(center, 1, 1) + south * pltpu.roll(center, lats - 1, 1))
                    if last:
                        y_ref[m, k, row - 8 : row] = value
                    else:
                        dst[k, row : row + 8] = value

    units = members + 1

    @pl.loop(0, units + LAG + HALO_LAG)
    def _(step):
        @pl.when(step < units)
        def _():
            @pl.when(jnp.logical_and(middle, d == 1))
            def _():
                r_forward(step)

            @pl.when(jnp.logical_and(middle, d == 2))
            def _():
                q_forward(step)

        unit = step - LAG

        @pl.when(jnp.logical_and(unit >= 0, unit < units))
        def _():
            @pl.when(d == 0)
            def _():
                q_wait(unit)

            @pl.when(d == n_lev - 1)
            def _():
                r_wait(unit)

            @pl.when(jnp.logical_and(middle, d == 1))
            def _():
                q_forward(unit)

            @pl.when(jnp.logical_and(middle, d == 2))
            def _():
                r_forward(unit)

            @pl.when(unit > 0)
            def _():
                finish(unit - 1)

        done = step - LAG - HALO_LAG - 1

        @pl.when(done >= 0)
        def _():
            diffuse(done)

    @pl.loop(0, units)
    def _(u):
        @pl.when(has_high)
        def _():
            r_copy(u, rout.at[u]).wait_send()

        @pl.when(has_low)
        def _():
            q_copy(u, qout.at[u]).wait_send()

    @pl.loop(0, members)
    def _(m):
        @pl.when(has_left)
        def _():
            left_copy(m).wait_send()

        @pl.when(has_right)
        def _():
            right_copy(m).wait_send()

    @pl.when(has_left)
    def _():
        kleft_copy().wait_send()

    @pl.when(has_right)
    def _():
        kright_copy().wait_send()


def write_kernel(y_ref, out_hbm, sems):
    members = y_ref.shape[0]
    copies = [pltpu.make_async_copy(y_ref.at[m], out_hbm.at[:, m], sems.at[m]) for m in range(members)]
    for copy in copies:
        copy.start()
    for copy in copies:
        copy.wait()


def solution(mesh):
    n_lev, n_col = mesh.shape["lev"], mesh.shape["col"]

    def per_device(control_field, decay_rate, diffusivity):
        levels, members, lons, lats = control_field.shape
        units = members + 1
        f32 = jnp.float32
        vmem = lambda *shape: pltpu.VMEM(shape, f32)
        dma = lambda *shape: pltpu.SemaphoreType.DMA(shape)
        state = (lons, lats)
        halo = (SMOOTH * levels, lats)
        y = pl.pallas_call(
            functools.partial(kernel, n_lev, n_col),
            out_shape=pltpu.VMEM((members, levels, lons, lats), f32),
            in_specs=[pl.BlockSpec(memory_space=pltpu.HBM), pl.BlockSpec(memory_space=pltpu.HBM), pl.BlockSpec(memory_space=pltpu.VMEM)],
            out_specs=pl.BlockSpec(memory_space=pltpu.VMEM),
            scratch_shapes=[
                vmem(levels, *state), vmem(levels, *state), vmem(4, levels, *state), vmem(6, *state), vmem(members, 4, *state),
                vmem(units, 2, *state), vmem(units, 2, *state), vmem(units, 2, *state), vmem(units, 2, *state),
                vmem(members, 2, *halo), vmem(members, 2, *halo),
                vmem(members, levels, lons + 16, lats), vmem(levels, lons + 16, lats),
                vmem(2, 8, lats), vmem(2, 8, lats), vmem(lons + 16, lats), vmem(3, lons + 16, lats),
                dma(), dma(members), dma(units), dma(units), dma(units), dma(units),
                dma(members, 2), dma(members, 2), dma(2), dma(2),
            ],
            compiler_params=pltpu.CompilerParams(collective_id=0, has_side_effects=True, vmem_limit_bytes=48 * 2**20),
        )(control_field, decay_rate, diffusivity)
        return pl.pallas_call(
            write_kernel,
            out_shape=jax.ShapeDtypeStruct(control_field.shape, f32),
            in_specs=[pl.BlockSpec(memory_space=pltpu.VMEM)],
            out_specs=pl.BlockSpec(memory_space=pl.ANY),
            scratch_shapes=[dma(members)],
            compiler_params=pltpu.CompilerParams(vmem_limit_bytes=8 * 2**20),
        )(y)

    in_specs = (P("lev", None, "col", None), P("lev", "col", None), P("col", None))
    return jax.shard_map(per_device, mesh=mesh, in_specs=in_specs, out_specs=P("lev", None, "col", None), check_vma=False)
```

time: 232 us -> 37.9 us (0.16)
  other arithmetic: 107 us -> 0 us
  local copies, waits for them, and re-layouts: 43 us -> 1.67 us
  Pallas kernels: 0 us -> 36 us
  starting transfers between devices: 34.4 us -> 0 us
  waiting for transfers between devices: 33.2 us -> 0 us
  blocking collectives: 10.9 us -> 0 us
    while x66 -> x0, other arithmetic: 70.6 us -> none
    pallas_call x0 -> x2, Pallas kernels: none -> 36 us  [the longest x1 33.7 us: per_device(): pl.pallas_call(functools.partial(kernel, n_lev, n_col), out_shape=pltpu.V...]
    all_to_all x4 -> x0, waiting for transfers between devices: 27.6 us -> none  [sent_to_all(): lax.all_to_all(jnp.broadcast_to(x[None], (peers, *x.shape)), axis, 0, 0,...]
    add x12 -> x0, other arithmetic: 26.1 us -> none  [the longest x4 12 us: per_device(): center + kappa_part[None, None] * (current[:, :, 2:] + current[:, :, :-2]...]
    ppermute x4 -> x0, starting transfers between devices: 18.9 us -> none  [the longest x2 14.9 us: with_halo(): lax.ppermute(lax.slice_in_dim(block, block.shape[dim] - width, None, axis...]
    dynamic_update_slice x12 -> x0, local copies, waits for them, and re-layouts: 15.7 us -> none  [sweep_levels(): lax.scan(run_block, start, (rate_blocks, field_blocks), reverse=backward)]
    all_to_all x4 -> x0, starting transfers between devices: 15.4 us -> none  [sent_to_all(): lax.all_to_all(jnp.broadcast_to(x[None], (peers, *x.shape)), axis, 0, 0,...]
    another operation x10 -> x0, local copies, waits for them, and re-layouts: 11 us -> none
  transfers between devices with their start and end apart: 8 -> 0, of which waited for: 4 -> 0; matrix products, arithmetic and copies ran while one was open for 15% -> 0% of each run, Pallas kernels for 0% -> 0%
where the time goes in v1:
time: 37.9 us; the launch traced here: 37.7 us
  Pallas kernels  36 us (95%)
  local copies, waits for them, and re-layouts  1.67 us (4%)
    pallas_call x1, Pallas kernels, per_device(): pl.pallas_call(functools.partial(kernel, n_lev, n_col), out_shape=pltpu.V...  33.7 us
    pallas_call x1, Pallas kernels, per_device(): pl.pallas_call(write_kernel, out_shape=jax.ShapeDtypeStruct(control_field...  2.31 us
    unnamed x4, local copies, waits for them, and re-layouts  1.67 us

profile of v1, /device:TPU:7, one launch (start us, length us, event | category | flops | bytes accessed | tf_op | source)
XLA Modules:
  0.0 37.7 jit_solution(17226010793210446948)
XLA Ops:
  0.0 0.0 copy-start
  0.0 1.0 %copy-done = f32[24,24,128]{2,1,0:T(8,128)S(1)} copy-done((f32[24,24,128]{2,1,0:T(8,128)S(1)}, f32[24,24,128]{2,1,0:T(8,128)}, u32[]{:S(2)}) %copy-start) | copy-done | bytes 294936
  1.0 0.0 copy-start.1
  1.0 0.7 %copy-done.1 = f32[24,128]{1,0:T(8,128)S(1)} copy-done((f32[24,128]{1,0:T(8,128)S(1)}, f32[24,128]{1,0:T(8,128)}, u32[]{:S(2)}) %copy-start.1) | copy-done | bytes 12312
  1.7 33.7 %shard_map.37.y_ref = f32[16,24,24,128]{3,2,1,0:T(8,128)S(1)} custom-call(f32[24,16,24,128]{3,2,1,0:T(8,128)} %x_hbm.1, f32[24,24,128]{2,1,0:T(8,128)S(1)} %copy-done, f32[24,128]{1,0:T(8,128)S(1)} %copy-done.1), custom_call_target="tpu_custom_call" | custom-call | tf_op jit(solution)/shard_map/pallas_call | solution.py:380
  35.4 2.3 %shard_map.38 = f32[24,16,24,128]{3,2,1,0:T(8,128)} custom-call(f32[16,24,24,128]{3,2,1,0:T(8,128)S(1)} %shard_map.37.y_ref), custom_call_target="tpu_custom_call" | custom-call | tf_op jit(solution)/shard_map/pallas_call | solution.py:396
Async XLA Ops:
  0.0 1.0 %copy-start = (f32[24,24,128]{2,1,0:T(8,128)S(1)}, f32[24,24,128]{2,1,0:T(8,128)}, u32[]{:S(2)}) copy-start(f32[24,24,128]{2,1,0:T(8,128)} %w_hbm.1) | copy-start | bytes 884740
  1.0 0.7 %copy-start.1 = (f32[24,128]{1,0:T(8,128)S(1)}, f32[24,128]{1,0:T(8,128)}, u32[]{:S(2)}) copy-start(f32[24,128]{1,0:T(8,128)} %kap_ref.1) | copy-start | bytes 36868

commit v2 on v1

--- a/solution.py
+++ b/solution.py
@@ -14,8 +14,46 @@
 HALO_LAG = 6
 
 
-def kernel(n_lev, n_col, x_hbm, w_hbm, kap_ref, y_ref, wv, bv, G, C, E, rin, rout, qin, qout, hs, hin, U, T, ks, kin, kw,
-           kc, wsem, xsem, rsend, rrecv, qsend, qrecv, hsend, hrecv, ksend, krecv):
+def diffuse(fields, put_last, ksh, tri, TT, levels, lons, lats):
+    for s in range(SMOOTH):
+        last = s == SMOOTH - 1
+        for t in range(lons // 8 + (0 if last else 1)):
+            for q in range(PAIR):
+                src = fields[q] if s == 0 else TT[s - 1].at[q]
+                first = (8 - SMOOTH if s == 0 else 0) + 8 * t
+                both = ksh[s, 8 * t : 8 * t + 8]
+                west, mid, east = (pl.ds(first + j, 8) for j in range(3))
+
+                def put(k, value):
+                    if last:
+                        put_last(q, k, t, value)
+                    else:
+                        TT[s][q, k, 8 * t : 8 * t + 8] = value
+
+                if q % 2:
+                    lane = lax.broadcasted_iota(jnp.int32, both.shape, 1)
+                    keep, north, south = 1.0 - 4.0 * both, jnp.where(lane > 0, both, 0.0), jnp.where(lane < lats - 1, both, 0.0)
+                    for k in range(levels):
+                        center = src[k, mid]
+                        sides = north * pltpu.roll(center, 1, 1) + south * pltpu.roll(center, lats - 1, 1)
+                        put(k, keep * center + both * (src[k, west] + src[k, east]) + sides)
+                else:
+                    center = src[:, mid].reshape(levels * 8, lats)
+                    high = center.astype(jnp.bfloat16)
+                    low = (center - high.astype(jnp.float32)).astype(jnp.bfloat16)
+                    sides = jnp.dot(jnp.concatenate([high, low], axis=1), tri[...], preferred_element_type=jnp.float32)
+                    sides = sides.reshape(levels, 8, lats)
+                    for k in range(levels):
+                        put(k, src[k, mid] + both * ((src[k, west] + src[k, east]) + sides[k]))
+
+
+def second_difference(tri, lats):
+    away = jnp.abs(lax.broadcasted_iota(jnp.int32, tri.shape, 0) % lats - lax.broadcasted_iota(jnp.int32, tri.shape, 1))
+    tri[...] = jnp.where(away == 0, -4.0, jnp.where(away == 1, 1.0, 0.0)).astype(jnp.bfloat16)
+
+
+def kernel(n_lev, n_col, x_hbm, w_hbm, kap_hbm, y_ref, U, ksh, kap_ref, wv, bv, G, C, E, rin, rout, qin, qout, hs, hin, TT, ks, kin, kw,
+           tri, wsem, kapsem, xsem, rsend, rrecv, qsend, qrecv, hsend, hrecv, ksend, krecv):
     levels, members, lons, lats = x_hbm.shape
     d, c = lax.axis_index("lev"), lax.axis_index("col")
     has_low, has_high = d > 0, d < n_lev - 1
@@ -30,6 +68,8 @@
 
     w_copy = pltpu.make_async_copy(w_hbm, wv, wsem)
     w_copy.start()
+    kap_copy = pltpu.make_async_copy(kap_hbm, kap_ref, kapsem)
+    kap_copy.start()
 
     def x_copy(m):
         return pltpu.make_async_copy(x_hbm.at[:, m], y_ref.at[m], xsem.at[m])
@@ -73,6 +113,7 @@
         kin[1] = jnp.zeros(kin.shape[1:], jnp.float32)
         hin[:, 1] = jnp.zeros((members,) + hin.shape[2:], jnp.float32)
 
+    kap_copy.wait()
     ks[...] = jnp.zeros_like(ks)
     ks[0, 0:SMOOTH] = kap_ref[0:SMOOTH]
     ks[1, 0:SMOOTH] = kap_ref[lons - SMOOTH : lons]
@@ -171,11 +212,9 @@
     kw[8 - SMOOTH : 8] = kin[0, 0:SMOOTH]
     kw[8 : 8 + lons] = kap_ref[...]
     kw[8 + lons : 8 + lons + SMOOTH] = kin[1, 0:SMOOTH]
-    kappa = kw[...]
-    lane = lax.broadcasted_iota(jnp.int32, kappa.shape, 1)
-    kc[0] = 1.0 - 4.0 * kappa
-    kc[1] = jnp.where(lane > 0, kappa, 0.0)
-    kc[2] = jnp.where(lane < lats - 1, kappa, 0.0)
+    for s in range(SMOOTH):
+        ksh[s] = kw[8 - SMOOTH + 1 + s : 8 - SMOOTH + 1 + s + lons + 8]
+    second_difference(tri, lats)
 
     def r_wait(u):
         r_copy(u, rout.at[u]).wait_recv()
@@ -254,7 +293,7 @@
         def _():
             right_copy(m).start()
 
-    def diffuse(m):
+    def take_halo(m):
         @pl.when(has_left)
         def _():
             pltpu.make_async_remote_copy(hs.at[m, 1], hin.at[m, 0], hsend.at[m, 1], hrecv.at[m, 0], device_id={"col": c - 1}, device_id_type=MESH).wait_recv()
@@ -266,24 +305,6 @@
         for k in range(levels):
             U[m, k, 8 - SMOOTH : 8] = hin[m, 0, SMOOTH * k : SMOOTH * (k + 1)]
             U[m, k, 8 + lons : 8 + lons + SMOOTH] = hin[m, 1, SMOOTH * k : SMOOTH * (k + 1)]
-        for s in range(SMOOTH):
-            src = U.at[m] if s % 2 == 0 else T
-            dst = T if s % 2 == 0 else U.at[m]
-            last = s == SMOOTH - 1
-            start = 8 - SMOOTH + 1 + s
-            tiles = lons // 8 + (0 if last else 1)
-            for t in range(tiles):
-                row = start + 8 * t
-                keep, north, south, both = kc[0, row : row + 8], kc[1, row : row + 8], kc[2, row : row + 8], kw[row : row + 8]
-                for k in range(levels):
-                    center = src[k, row : row + 8]
-                    value = keep * center + both * (src[k, row - 1 : row + 7] + src[k, row + 1 : row + 9])
-                    value = value + (north * pltpu.roll(center, 1, 1) + south * pltpu.roll(center, lats - 1, 1))
-                    if last:
-                        y_ref[m, k, row - 8 : row] = value
-                    else:
-                        dst[k, row : row + 8] = value
-
     units = members + 1
 
     @pl.loop(0, units + LAG + HALO_LAG)
@@ -326,7 +347,16 @@
 
         @pl.when(done >= 0)
         def _():
-            diffuse(done)
+            take_halo(done)
+
+        @pl.when(jnp.logical_and(jnp.logical_and(done >= 0, done < members - PAIR), done % PAIR == PAIR - 1))
+        def _():
+            m = done - (PAIR - 1)
+
+            def put_last(q, k, t, value):
+                y_ref[m + q, k, 8 * t : 8 * t + 8] = value
+
+            diffuse([U.at[m + q] for q in range(PAIR)], put_last, ksh, tri, TT, levels, lons, lats)
 
     @pl.loop(0, units)
     def _(u):
@@ -357,10 +387,20 @@
         kright_copy().wait_send()
 
 
-def write_kernel(y_ref, out_hbm, sems):
-    members = y_ref.shape[0]
-    copies = [pltpu.make_async_copy(y_ref.at[m], out_hbm.at[:, m], sems.at[m]) for m in range(members)]
-    for copy in copies:
+def write_kernel(y_ref, U, ksh, out_hbm, tri, y_last, TT, sems):
+    members, levels, lons, lats = y_ref.shape
+    early = members - PAIR
+    copies = [pltpu.make_async_copy(y_ref.at[m], out_hbm.at[:, m], sems.at[m]) for m in range(early)]
+    copies += [pltpu.make_async_copy(y_last.at[q], out_hbm.at[:, early + q], sems.at[early + q]) for q in range(PAIR)]
+    for copy in copies[:early]:
+        copy.start()
+    second_difference(tri, lats)
+
+    def put_last(q, k, t, value):
+        y_last[q, k, 8 * t : 8 * t + 8] = value
+
+    diffuse([U.at[early + q] for q in range(PAIR)], put_last, ksh, tri, TT, levels, lons, lats)
+    for copy in copies[early:]:
         copy.start()
     for copy in copies:
         copy.wait()
@@ -377,30 +417,33 @@
         dma = lambda *shape: pltpu.SemaphoreType.DMA(shape)
         state = (lons, lats)
         halo = (SMOOTH * levels, lats)
-        y = pl.pallas_call(
+        steps = [vmem(PAIR, levels, lons + 16, lats)] * (SMOOTH - 1)
+        triangle = pltpu.VMEM((2 * lats, lats), jnp.bfloat16)
+        in_vmem = pl.BlockSpec(memory_space=pltpu.VMEM)
+        y, wide, kappas = pl.pallas_call(
             functools.partial(kernel, n_lev, n_col),
-            out_shape=pltpu.VMEM((members, levels, lons, lats), f32),
-            in_specs=[pl.BlockSpec(memory_space=pltpu.HBM), pl.BlockSpec(memory_space=pltpu.HBM), pl.BlockSpec(memory_space=pltpu.VMEM)],
-            out_specs=pl.BlockSpec(memory_space=pltpu.VMEM),
+            out_shape=[vmem(members, levels, lons, lats), vmem(members, levels, lons + 16, lats), vmem(SMOOTH, lons + 8, lats)],
+            in_specs=[pl.BlockSpec(memory_space=pltpu.HBM), pl.BlockSpec(memory_space=pltpu.HBM), pl.BlockSpec(memory_space=pltpu.HBM)],
+            out_specs=[in_vmem] * 3,
             scratch_shapes=[
-                vmem(levels, *state), vmem(levels, *state), vmem(4, levels, *state), vmem(6, *state), vmem(members, 4, *state),
+                vmem(*state), vmem(levels, *state), vmem(levels, *state), vmem(4, levels, *state), vmem(6, *state), vmem(members, 4, *state),
                 vmem(units, 2, *state), vmem(units, 2, *state), vmem(units, 2, *state), vmem(units, 2, *state),
                 vmem(members, 2, *halo), vmem(members, 2, *halo),
-                vmem(members, levels, lons + 16, lats), vmem(levels, lons + 16, lats),
-                vmem(2, 8, lats), vmem(2, 8, lats), vmem(lons + 16, lats), vmem(3, lons + 16, lats),
-                dma(), dma(members), dma(units), dma(units), dma(units), dma(units),
+                steps,
+                vmem(2, 8, lats), vmem(2, 8, lats), vmem(lons + 16, lats), triangle,
+                dma(), dma(), dma(members), dma(units), dma(units), dma(units), dma(units),
                 dma(members, 2), dma(members, 2), dma(2), dma(2),
             ],
-            compiler_params=pltpu.CompilerParams(collective_id=0, has_side_effects=True, vmem_limit_bytes=48 * 2**20),
-        )(control_field, decay_rate, diffusivity)
+            compiler_params=pltpu.CompilerParams(collective_id=0, has_side_effects=True, vmem_limit_bytes=32 * 2**20),
+        )(*(pltpu.with_memory_space_constraint(x, pltpu.HBM) for x in (control_field, decay_rate, diffusivity)))
         return pl.pallas_call(
             write_kernel,
             out_shape=jax.ShapeDtypeStruct(control_field.shape, f32),
-            in_specs=[pl.BlockSpec(memory_space=pltpu.VMEM)],
+            in_specs=[in_vmem] * 3,
             out_specs=pl.BlockSpec(memory_space=pl.ANY),
-            scratch_shapes=[dma(members)],
-            compiler_params=pltpu.CompilerParams(vmem_limit_bytes=8 * 2**20),
-        )(y)
+            scratch_shapes=[triangle, vmem(PAIR, levels, lons, lats), steps, dma(members)],
+            compiler_params=pltpu.CompilerParams(vmem_limit_bytes=12 * 2**20),
+        )(y, wide, kappas)
 
     in_specs = (P("lev", None, "col", None), P("lev", "col", None), P("col", None))
     return jax.shard_map(per_device, mesh=mesh, in_specs=in_specs, out_specs=P("lev", None, "col", None), check_vma=False)

time: 37.9 us -> 32.7 us (0.86)
  Pallas kernels: 36 us -> 32.2 us
  local copies, waits for them, and re-layouts: 1.67 us -> 0 us
    pallas_call x1, Pallas kernels: 33.7 us -> 29.2 us  [per_device(): pl.pallas_call(functools.partial(kernel, n_lev, n_col), out_shape=[vmem(m...]
    unnamed x4 -> x0, local copies, waits for them, and re-layouts: 1.67 us -> none
    pallas_call x1, Pallas kernels: 2.31 us -> 2.99 us  [per_device(): pl.pallas_call(write_kernel, out_shape=jax.ShapeDtypeStruct(control_field...]
where the time goes in v2:
time: 32.7 us; the launch traced here: 32.2 us
  Pallas kernels  32.2 us (98%)
    pallas_call x1, Pallas kernels, per_device(): pl.pallas_call(functools.partial(kernel, n_lev, n_col), out_shape=[vmem(m...  29.2 us
    pallas_call x1, Pallas kernels, per_device(): pl.pallas_call(write_kernel, out_shape=jax.ShapeDtypeStruct(control_field...  2.99 us

profile of v2, /device:TPU:7, one launch (start us, length us, event | category | flops | bytes accessed | tf_op | source)
XLA Modules:
  0.0 32.2 jit_solution(13136982657304911522)
XLA Ops:
  0.0 29.2 %shard_map.37 = (f32[16,24,24,128]{3,2,1,0:T(8,128)S(1)}, f32[16,24,40,128]{3,2,1,0:T(8,128)S(1)}, f32[4,32,128]{2,1,0:T(8,128)S(1)}) custom-call(f32[24,16,24,128]{3,2,1,0:T(8,128)} %x_hbm.1, f32[24,24,128]{2,1,0:T(8,128)} %w_hbm.1, f32[24,128]{1,0:T(8,128)} %kap_hbm.1), custom_call_target="tpu_custom_call" | custom-call | tf_op jit(solution)/shard_map/pallas_call | solution.py:423
  29.2 3.0 %shard_map.38 = f32[24,16,24,128]{3,2,1,0:T(8,128)} custom-call(f32[16,24,24,128]{3,2,1,0:T(8,128)S(1)} %get-tuple-element.8.y_ref, f32[16,24,40,128]{3,2,1,0:T(8,128)S(1)} %get-tuple-element.9.U, f32[4,32,128]{2,1,0:T(8,128)S(1)} %get-tuple-element.10.ksh), custom_call_target="tpu_custom_call" | custom-call | tf_op jit(solution)/shard_map/pallas_call | solution.py:439

commit v3 on v2

--- a/solution.py
+++ b/solution.py
@@ -11,7 +11,8 @@
 SMOOTH = 4
 PAIR = 2
 LAG = 6
-HALO_LAG = 6
+HALO_LAG = 7
+LATER = 6
 
 
 def diffuse(fields, put_last, ksh, tri, TT, levels, lons, lats):
@@ -30,9 +31,10 @@
                     else:
                         TT[s][q, k, 8 * t : 8 * t + 8] = value
 
+                keep = 1.0 - 4.0 * both
                 if q % 2:
                     lane = lax.broadcasted_iota(jnp.int32, both.shape, 1)
-                    keep, north, south = 1.0 - 4.0 * both, jnp.where(lane > 0, both, 0.0), jnp.where(lane < lats - 1, both, 0.0)
+                    north, south = jnp.where(lane > 0, both, 0.0), jnp.where(lane < lats - 1, both, 0.0)
                     for k in range(levels):
                         center = src[k, mid]
                         sides = north * pltpu.roll(center, 1, 1) + south * pltpu.roll(center, lats - 1, 1)
@@ -44,12 +46,12 @@
                     sides = jnp.dot(jnp.concatenate([high, low], axis=1), tri[...], preferred_element_type=jnp.float32)
                     sides = sides.reshape(levels, 8, lats)
                     for k in range(levels):
-                        put(k, src[k, mid] + both * ((src[k, west] + src[k, east]) + sides[k]))
-
-
-def second_difference(tri, lats):
+                        put(k, keep * src[k, mid] + both * ((src[k, west] + src[k, east]) + sides[k]))
+
+
+def neighbours(tri, lats):
     away = jnp.abs(lax.broadcasted_iota(jnp.int32, tri.shape, 0) % lats - lax.broadcasted_iota(jnp.int32, tri.shape, 1))
-    tri[...] = jnp.where(away == 0, -4.0, jnp.where(away == 1, 1.0, 0.0)).astype(jnp.bfloat16)
+    tri[...] = jnp.where(away == 1, 1.0, 0.0).astype(jnp.bfloat16)
 
 
 def kernel(n_lev, n_col, x_hbm, w_hbm, kap_hbm, y_ref, U, ksh, kap_ref, wv, bv, G, C, E, rin, rout, qin, qout, hs, hin, TT, ks, kin, kw,
@@ -74,7 +76,7 @@
     def x_copy(m):
         return pltpu.make_async_copy(x_hbm.at[:, m], y_ref.at[m], xsem.at[m])
 
-    for m in range(members):
+    for m in range(PAIR):
         x_copy(m).start()
 
     def r_copy(u, src):
@@ -119,6 +121,8 @@
     ks[1, 0:SMOOTH] = kap_ref[lons - SMOOTH : lons]
 
     w_copy.wait()
+    for m in range(PAIR, members):
+        x_copy(m).start()
     state = jnp.ones((lons, lats), jnp.float32)
     for k in range(levels):
         bv[k] = 1.0 - wv[k]
@@ -214,7 +218,7 @@
     kw[8 + lons : 8 + lons + SMOOTH] = kin[1, 0:SMOOTH]
     for s in range(SMOOTH):
         ksh[s] = kw[8 - SMOOTH + 1 + s : 8 - SMOOTH + 1 + s + lons + 8]
-    second_difference(tri, lats)
+    neighbours(tri, lats)
 
     def r_wait(u):
         r_copy(u, rout.at[u]).wait_recv()
@@ -307,7 +311,7 @@
             U[m, k, 8 + lons : 8 + lons + SMOOTH] = hin[m, 1, SMOOTH * k : SMOOTH * (k + 1)]
     units = members + 1
 
-    @pl.loop(0, units + LAG + HALO_LAG)
+    @pl.loop(0, units + LAG + HALO_LAG + LATER)
     def _(step):
         @pl.when(step < units)
         def _():
@@ -343,9 +347,9 @@
             def _():
                 finish(unit - 1)
 
-        done = step - LAG - HALO_LAG - 1
-
-        @pl.when(done >= 0)
+        done = step - LAG - HALO_LAG - 1 - jnp.where(middle, LATER, 0)
+
+        @pl.when(jnp.logical_and(done >= 0, done < members))
         def _():
             take_halo(done)
 
@@ -394,7 +398,7 @@
     copies += [pltpu.make_async_copy(y_last.at[q], out_hbm.at[:, early + q], sems.at[early + q]) for q in range(PAIR)]
     for copy in copies[:early]:
         copy.start()
-    second_difference(tri, lats)
+    neighbours(tri, lats)
 
     def put_last(q, k, t, value):
         y_last[q, k, 8 * t : 8 * t + 8] = value

time: 32.7 us -> 31.3 us (0.957)
  Pallas kernels: 32.2 us -> 31.1 us
    pallas_call x1, Pallas kernels: 29.2 us -> 28.1 us  [per_device(): pl.pallas_call(functools.partial(kernel, n_lev, n_col), out_shape=[vmem(m...]
where the time goes in v3:
time: 31.3 us; the launch traced here: 31.1 us
  Pallas kernels  31.1 us (99%)
    pallas_call x1, Pallas kernels, per_device(): pl.pallas_call(functools.partial(kernel, n_lev, n_col), out_shape=[vmem(m...  28.1 us
    pallas_call x1, Pallas kernels, per_device(): pl.pallas_call(write_kernel, out_shape=jax.ShapeDtypeStruct(control_field...  3.02 us

profile of v3, /device:TPU:7, one launch (start us, length us, event | category | flops | bytes accessed | tf_op | source)
XLA Modules:
  0.0 31.1 jit_solution(16156123621511789490)
XLA Ops:
  0.0 28.1 %shard_map.37 = (f32[16,24,24,128]{3,2,1,0:T(8,128)S(1)}, f32[16,24,40,128]{3,2,1,0:T(8,128)S(1)}, f32[4,32,128]{2,1,0:T(8,128)S(1)}) custom-call(f32[24,16,24,128]{3,2,1,0:T(8,128)} %x_hbm.1, f32[24,24,128]{2,1,0:T(8,128)} %w_hbm.1, f32[24,128]{1,0:T(8,128)} %kap_hbm.1), custom_call_target="tpu_custom_call" | custom-call | tf_op jit(solution)/shard_map/pallas_call | solution.py:427
  28.1 3.0 %shard_map.38 = f32[24,16,24,128]{3,2,1,0:T(8,128)} custom-call(f32[16,24,24,128]{3,2,1,0:T(8,128)S(1)} %get-tuple-element.8.y_ref, f32[16,24,40,128]{3,2,1,0:T(8,128)S(1)} %get-tuple-element.9.U, f32[4,32,128]{2,1,0:T(8,128)S(1)} %get-tuple-element.10.ksh), custom_call_target="tpu_custom_call" | custom-call | tf_op jit(solution)/shard_map/pallas_call | solution.py:443
